TPU v7x, 8 devices: a whole 2x2x1 slice. The times are simulated.
8 devices in a mesh: data: 2 (over z, y), stage: 4 (over x, core).
Axes of the slice: x: 2, y: 2, z: 1, core: 2. Of those that a mesh axis runs over, the one named last changes fastest.
Arguments:
- acts_in: bfloat16 [16, 4096, 768], P(('data', 'stage')), parts along dimension 0
- grad_out: bfloat16 [16, 4096, 768], P(('data', 'stage')), parts along dimension 0
- w_up_a: bfloat16 [4, 768, 3072], P('stage')
- w_down_a: bfloat16 [4, 3072, 768], P('stage')
- w_up_b: bfloat16 [4, 768, 768], P('stage')
- w_down_b: bfloat16 [4, 768, 768], P('stage')
Outputs:
- output 1: bfloat16 [16, 4096, 768], P(('data', 'stage')), parts along dimension 0
- output 2: bfloat16 [16, 4096, 768], P(('data', 'stage')), parts along dimension 0
- output 3: float32 [8, 768, 3072], P(('data', 'stage')), parts along dimension 0
- output 4: float32 [8, 3072, 768], P(('data', 'stage')), parts along dimension 0
- output 5: float32 [8, 768, 768], P(('data', 'stage')), parts along dimension 0
- output 6: float32 [8, 768, 768], P(('data', 'stage')), parts along dimension 0
There are 2 independent parts. A program takes and returns all parts, laid end to end along the dimension named above; an argument that names none is the same for every part.
All inputs are finite; a program needn't handle non-finite values.
Results may differ from a plain program's by a relative error of at most 0.0163569.
Values are sent between devices in bfloat16 or wider.
A program may use at most 1 GiB of HBM per device.

v0:
```python
import jax
import jax.numpy as jnp
from jax import lax
from jax.sharding import PartitionSpec as P


def layer_forward(hidden, w_up, w_down):
    pre_act = jnp.dot(hidden, w_up, preferred_element_type=jnp.float32)
    gelu_out = jax.nn.gelu(pre_act).astype(jnp.bfloat16)
    resid_delta = jnp.dot(gelu_out, w_down, preferred_element_type=jnp.float32)
    return (hidden.astype(jnp.float32) + resid_delta).astype(jnp.bfloat16)


def layer_backward(hidden, w_up, w_down, grad_next):
    pre_act = jnp.dot(hidden, w_up, preferred_element_type=jnp.float32)
    gelu_val, gelu_pull = jax.vjp(jax.nn.gelu, pre_act)
    gelu_out = gelu_val.astype(jnp.bfloat16)
    dw_down = jnp.einsum('tf,td->fd', gelu_out, grad_next, preferred_element_type=jnp.float32)
    d_gelu = jnp.einsum('td,fd->tf', grad_next, w_down, preferred_element_type=jnp.float32)
    d_pre = gelu_pull(d_gelu)[0].astype(jnp.bfloat16)
    dw_up = jnp.einsum('td,tf->df', hidden, d_pre, preferred_element_type=jnp.float32)
    back_prod = jnp.einsum('tf,df->td', d_pre, w_up, preferred_element_type=jnp.float32)
    grad_prev = (grad_next.astype(jnp.float32) + back_prod).astype(jnp.bfloat16)
    return grad_prev, dw_up, dw_down


def pair_forward(hidden, pair_weights):
    up_a, down_a, up_b, down_b = pair_weights
    mid_hidden = layer_forward(hidden, up_a, down_a)
    return layer_forward(mid_hidden, up_b, down_b), (hidden, mid_hidden)


def pair_backward(grad_next, step_in):
    (hidden, mid_hidden), (up_a, down_a, up_b, down_b) = step_in
    grad_mid, dw_up_b, dw_down_b = layer_backward(mid_hidden, up_b, down_b, grad_next)
    grad_prev, dw_up_a, dw_down_a = layer_backward(hidden, up_a, down_a, grad_mid)
    return grad_prev, (dw_up_a, dw_down_a, dw_up_b, dw_down_b)


def gather_round(local_rows, round_idx):
    return tuple(lax.all_gather(weight[round_idx], 'stage') for weight in local_rows)


def solution(mesh):
    tok_spec = P(('data', 'stage'))
    row_spec = P('stage')

    def device_body(acts_in, grad_out, w_up_a, w_down_a, w_up_b, w_down_b):
        n_micro, tokens, model_width = acts_in.shape
        local_rows = (w_up_a, w_down_a, w_up_b, w_down_b)
        num_rounds = w_up_a.shape[0]
        hidden = acts_in.reshape(n_micro * tokens, model_width)
        saved_acts = []
        for round_idx in range(num_rounds):
            hidden, round_saved = lax.scan(pair_forward, hidden, gather_round(local_rows, round_idx))
            saved_acts.append(round_saved)
        grad_h = grad_out.reshape(n_micro * tokens, model_width)
        round_grads = []
        for round_idx in reversed(range(num_rounds)):
            round_weights = gather_round(local_rows, round_idx)
            grad_h, pair_grads = lax.scan(pair_backward, grad_h, (saved_acts[round_idx], round_weights), reverse=True)
            round_grads.append(tuple(lax.psum_scatter(grad_stack, 'stage', scatter_dimension=0, tiled=True) for grad_stack in pair_grads))
        round_grads = round_grads[::-1]
        weight_grads = tuple(jnp.concatenate([round_set[slot_idx] for round_set in round_grads], axis=0) for slot_idx in range(4))
        return (hidden.reshape(acts_in.shape), grad_h.reshape(acts_in.shape)) + weight_grads

    return jax.shard_map(device_body, mesh=mesh, in_specs=(tok_spec, tok_spec, row_spec, row_spec, row_spec, row_spec), out_specs=(tok_spec,) * 6, check_vma=False)
```

profile of v0, /device:TPU:0, one launch (start us, length us, event | category | flops | bytes accessed | tf_op | source)
XLA Modules:
  0.0 3309.1 jit_solution(5915986967194170806)
XLA Ops:
  27.1 35.4 %all-gather.9.cloned.1.call-done = bf16[4,768,768]{2,1,0:T(8,128)(2,1)} async-done(((bf16[1,768,768]{2,1,0:T(8,128)(2,1)}), bf16[4,768,768]{2,1,0:T(8,128)(2,1)}) %all-gather.9.cloned.1.call-update) | async-done | bytes 4718608 | tf_op jit(solution)/shard_map/all_gather | solution.py:41
  62.5 36.1 %all-gather.11.cloned.1.call-done = bf16[4,768,768]{2,1,0:T(8,128)(2,1)} async-done(((bf16[1,768,768]{2,1,0:T(8,128)(2,1)}), bf16[4,768,768]{2,1,0:T(8,128)(2,1)}) %all-gather.11.cloned.1.call-update) | async-done | bytes 4718608 | tf_op jit(solution)/shard_map/all_gather | solution.py:41
  98.6 119.6 %all-gather.5.cloned.1.call-done = bf16[4,768,3072]{2,1,0:T(8,128)(2,1)} async-done(((bf16[1,768,3072]{2,1,0:T(8,128)(2,1)}), bf16[4,768,3072]{2,1,0:T(8,128)(2,1)}) %all-gather.5.cloned.1.call-update) | async-done | bytes 18874384 | tf_op jit(solution)/shard_map/all_gather | solution.py:41
  218.3 119.5 %all-gather.7.cloned.1.call-done = bf16[4,3072,768]{2,1,0:T(8,128)(2,1)} async-done(((bf16[1,3072,768]{2,1,0:T(8,128)(2,1)}), bf16[4,3072,768]{2,1,0:T(8,128)(2,1)}) %all-gather.7.cloned.1.call-update) | async-done | bytes 18874384 | tf_op jit(solution)/shard_map/all_gather | solution.py:41
  337.7 640.5 %while.37 = (s32[]{:T(128)}, bf16[8192,768]{1,0:T(8,128)(2,1)}, bf16[4,8192,768]{2,1,0:T(8,128)(2,1)}, bf16[4,8192,768]{2,1,0:T(8,128)(2,1)}, bf16[4,768,3072]{2...) while((s32[]{:T(128)}, bf16[8192,768]{1,0:T(8,128)(2,1)}, ...), condition=%wide.region_1.2_spmd, body=%wide.region_0.1_spmd.sunk | while | flops 96957628416 | bytes 225708144 | solution.py:55
  348.3 69.7 %fusion.7.clone.1.clone.7 = bf16[8192,3072]{0,1:T(8,128)(2,1)} fusion(bf16[8192,768]{1,0:T(8,128)(2,1)} %get-tuple-element.509, bf16[4,768,3072]{2,1,0:T(8,128)(2,1)} %get-tuple-element.521, s32[]{:T(128)S(6)} %copy.35), kind=kOutput, calls=%fused_computation.8.clone.clone.clone.clone.clone.2.clone.1 | convolution fusion | flops 38881198080 | bytes 67633152 | tf_op jit(solution)/shard_map/while/body/eval_jaxpr/dot_general | solution.py:8
  417.9 49.5 %bitcast_dynamic-update-slice_fusion.12 = (bf16[4,8192,768]{2,1,0:T(8,128)(2,1)}, bf16[8192,768]{1,0:T(8,128)(2,1)}) fusion(bf16[4,8192,768]{2,1,0:T(8,128)(2,1)} %get-tuple-element.511, s32[]{:T(128)S(6)} %copy.35, bf16[4,3072,768]{2,1,0:T(8,128)(2,1)} %get-tuple-element.522, bf16[8192,768]{1,0:T(8,128)(2,1)} %get-tuple-element.509, ...), kind=kOutput, calls=%fused_computation.20.clone.3 | convolution fusion | flops 38673580032 | bytes 92800000 | tf_op jit(solution)/shard_map/while/body/eval_jaxpr/dot_general | solution.py:10
  467.4 30.4 add_convert_fusion.7
  508.4 69.7 %fusion.7.clone.1.clone.7 = bf16[8192,3072]{0,1:T(8,128)(2,1)} fusion(bf16[8192,768]{1,0:T(8,128)(2,1)} %get-tuple-element.509, bf16[4,768,3072]{2,1,0:T(8,128)(2,1)} %get-tuple-element.521, s32[]{:T(128)S(6)} %copy.35), kind=kOutput, calls=%fused_computation.8.clone.clone.clone.clone.clone.2.clone.1 | convolution fusion | flops 38881198080 | bytes 67633152 | tf_op jit(solution)/shard_map/while/body/eval_jaxpr/dot_general | solution.py:8
  578.2 49.5 %bitcast_dynamic-update-slice_fusion.12 = (bf16[4,8192,768]{2,1,0:T(8,128)(2,1)}, bf16[8192,768]{1,0:T(8,128)(2,1)}) fusion(bf16[4,8192,768]{2,1,0:T(8,128)(2,1)} %get-tuple-element.511, s32[]{:T(128)S(6)} %copy.35, bf16[4,3072,768]{2,1,0:T(8,128)(2,1)} %get-tuple-element.522, bf16[8192,768]{1,0:T(8,128)(2,1)} %get-tuple-element.509, ...), kind=kOutput, calls=%fused_computation.20.clone.3 | convolution fusion | flops 38673580032 | bytes 92800000 | tf_op jit(solution)/shard_map/while/body/eval_jaxpr/dot_general | solution.py:10
  627.6 30.4 add_convert_fusion.7
  668.5 69.7 %fusion.7.clone.1.clone.7 = bf16[8192,3072]{0,1:T(8,128)(2,1)} fusion(bf16[8192,768]{1,0:T(8,128)(2,1)} %get-tuple-element.509, bf16[4,768,3072]{2,1,0:T(8,128)(2,1)} %get-tuple-element.521, s32[]{:T(128)S(6)} %copy.35), kind=kOutput, calls=%fused_computation.8.clone.clone.clone.clone.clone.2.clone.1 | convolution fusion | flops 38881198080 | bytes 67633152 | tf_op jit(solution)/shard_map/while/body/eval_jaxpr/dot_general | solution.py:8
  738.3 49.5 %bitcast_dynamic-update-slice_fusion.12 = (bf16[4,8192,768]{2,1,0:T(8,128)(2,1)}, bf16[8192,768]{1,0:T(8,128)(2,1)}) fusion(bf16[4,8192,768]{2,1,0:T(8,128)(2,1)} %get-tuple-element.511, s32[]{:T(128)S(6)} %copy.35, bf16[4,3072,768]{2,1,0:T(8,128)(2,1)} %get-tuple-element.522, bf16[8192,768]{1,0:T(8,128)(2,1)} %get-tuple-element.509, ...), kind=kOutput, calls=%fused_computation.20.clone.3 | convolution fusion | flops 38673580032 | bytes 92800000 | tf_op jit(solution)/shard_map/while/body/eval_jaxpr/dot_general | solution.py:10
  787.7 30.4 add_convert_fusion.7
  828.6 69.7 %fusion.7.clone.1.clone.7 = bf16[8192,3072]{0,1:T(8,128)(2,1)} fusion(bf16[8192,768]{1,0:T(8,128)(2,1)} %get-tuple-element.509, bf16[4,768,3072]{2,1,0:T(8,128)(2,1)} %get-tuple-element.521, s32[]{:T(128)S(6)} %copy.35), kind=kOutput, calls=%fused_computation.8.clone.clone.clone.clone.clone.2.clone.1 | convolution fusion | flops 38881198080 | bytes 67633152 | tf_op jit(solution)/shard_map/while/body/eval_jaxpr/dot_general | solution.py:8
  898.3 49.5 %bitcast_dynamic-update-slice_fusion.12 = (bf16[4,8192,768]{2,1,0:T(8,128)(2,1)}, bf16[8192,768]{1,0:T(8,128)(2,1)}) fusion(bf16[4,8192,768]{2,1,0:T(8,128)(2,1)} %get-tuple-element.511, s32[]{:T(128)S(6)} %copy.35, bf16[4,3072,768]{2,1,0:T(8,128)(2,1)} %get-tuple-element.522, bf16[8192,768]{1,0:T(8,128)(2,1)} %get-tuple-element.509, ...), kind=kOutput, calls=%fused_computation.20.clone.3 | convolution fusion | flops 38673580032 | bytes 92800000 | tf_op jit(solution)/shard_map/while/body/eval_jaxpr/dot_general | solution.py:10
  947.8 30.4 add_convert_fusion.7
  1012.1 1634.6 %while.38 = (s32[]{:T(128)}, bf16[8192,768]{1,0:T(8,128)(2,1)}, f32[4,768,3072]{2,1,0:T(8,128)}, f32[4,3072,768]{2,1,0:T(8,128)}, f32[4,768,768]{2,1,0:T(8,128)}...) while((s32[]{:T(128)}, bf16[8192,768]{1,0:T(8,128)(2,1)}, ...), condition=%wide.region_3.4_spmd, body=%wide.region_2.3_spmd.sunk | while | flops 242541920256 | bytes 808849600 | solution.py:61
  1036.9 24.7 bitcast_dynamic-update-slice_fusion.17
  1061.6 27.6 fusion.197
  1124.0 50.6 %fusion.198 = f32[8192,3072]{1,0:T(8,128)} fusion(bf16[4,8192,768]{2,1,0:T(8,128)(2,1)} %get-tuple-element.564, s32[]{:T(128)S(6)} %sub.35, bf16[4,768,3072]{2,1,0:T(8,128)(2,1)} %get-tuple-element.565), kind=kOutput, calls=%fused_computation.74.clone.3 | convolution fusion | flops 38654705664 | bytes 117965824 | tf_op jit(solution)/shard_map/while/body/eval_jaxpr/dot_general | solution.py:15
  1174.6 56.6 %bitcast_dynamic-update-slice_fusion.15 = f32[4,3072,768]{2,1,0:T(8,128)} fusion(f32[4,3072,768]{2,1,0:T(8,128)} %get-tuple-element.543, s32[]{:T(128)S(6)} %sub.35, bf16[8192,768]{1,0:T(8,128)(2,1)} %add_convert_fusion.8, f32[8192,3072]{1,0:T(8,128)} %fusion.198), kind=kOutput, calls=%fused_computation.85.clone.2 | convolution fusion | flops 38881198080 | bytes 122683392 | tf_op jit(solution)/shard_map/while/body/eval_jaxpr/tf,td->fd/dot_general | solution.py:18
  1231.3 98.1 %fusion.199 = bf16[8192,3072]{1,0:T(8,128)(2,1)} fusion(f32[8192,3072]{1,0:T(8,128)} %fusion.198, bf16[8192,768]{1,0:T(8,128)(2,1)} %add_convert_fusion.8, bf16[4,3072,768]{2,1,0:T(8,128)(2,1)} %get-tuple-element.563, s32[]{:T(128)S(6)} %sub.35), kind=kOutput, calls=%fused_computation.52.clone.2 | convolution fusion | flops 39158022144 | bytes 168296448 | tf_op jit(solution)/shard_map/while/body/eval_jaxpr/td,fd->tf/dot_general | solution.py:19
  1329.4 47.7 %add_convert_fusion.9 = bf16[8192,768]{1,0:T(8,128)(2,1)} fusion(bf16[8192,768]{1,0:T(8,128)(2,1)} %add_convert_fusion.8, bf16[8192,3072]{1,0:T(8,128)(2,1)} %fusion.199, bf16[4,768,3072]{2,1,0:T(8,128)(2,1)} %get-tuple-element.565, s32[]{:T(128)S(6)} %sub.35), kind=kOutput, calls=%fused_computation.70.clone.1 | convolution fusion | flops 38673580032 | bytes 80216064 | tf_op jit(solution)/shard_map/while/body/eval_jaxpr/tf,df->td/dot_general | solution.py:22
  1377.1 48.3 %bitcast_dynamic-update-slice_fusion.14 = f32[4,768,3072]{2,1,0:T(8,128)} fusion(f32[4,768,3072]{2,1,0:T(8,128)} %get-tuple-element.542, s32[]{:T(128)S(6)} %sub.35, bf16[8192,3072]{1,0:T(8,128)(2,1)} %fusion.199, bf16[4,8192,768]{2,1,0:T(8,128)(2,1)} %get-tuple-element.564), kind=kOutput, calls=%fused_computation.86.clone.1 | convolution fusion | flops 38654705664 | bytes 72352768 | tf_op jit(solution)/shard_map/while/body/eval_jaxpr/td,tf->df/dot_general | solution.py:21
  1443.7 24.7 bitcast_dynamic-update-slice_fusion.17
  1468.3 27.5 fusion.197
  1530.6 50.4 %fusion.198 = f32[8192,3072]{1,0:T(8,128)} fusion(bf16[4,8192,768]{2,1,0:T(8,128)(2,1)} %get-tuple-element.564, s32[]{:T(128)S(6)} %sub.35, bf16[4,768,3072]{2,1,0:T(8,128)(2,1)} %get-tuple-element.565), kind=kOutput, calls=%fused_computation.74.clone.3 | convolution fusion | flops 38654705664 | bytes 117965824 | tf_op jit(solution)/shard_map/while/body/eval_jaxpr/dot_general | solution.py:15
  1581.0 56.9 %bitcast_dynamic-update-slice_fusion.15 = f32[4,3072,768]{2,1,0:T(8,128)} fusion(f32[4,3072,768]{2,1,0:T(8,128)} %get-tuple-element.543, s32[]{:T(128)S(6)} %sub.35, bf16[8192,768]{1,0:T(8,128)(2,1)} %add_convert_fusion.8, f32[8192,3072]{1,0:T(8,128)} %fusion.198), kind=kOutput, calls=%fused_computation.85.clone.2 | convolution fusion | flops 38881198080 | bytes 122683392 | tf_op jit(solution)/shard_map/while/body/eval_jaxpr/tf,td->fd/dot_general | solution.py:18
  1637.9 98.1 %fusion.199 = bf16[8192,3072]{1,0:T(8,128)(2,1)} fusion(f32[8192,3072]{1,0:T(8,128)} %fusion.198, bf16[8192,768]{1,0:T(8,128)(2,1)} %add_convert_fusion.8, bf16[4,3072,768]{2,1,0:T(8,128)(2,1)} %get-tuple-element.563, s32[]{:T(128)S(6)} %sub.35), kind=kOutput, calls=%fused_computation.52.clone.2 | convolution fusion | flops 39158022144 | bytes 168296448 | tf_op jit(solution)/shard_map/while/body/eval_jaxpr/td,fd->tf/dot_general | solution.py:19
  1736.1 47.6 %add_convert_fusion.9 = bf16[8192,768]{1,0:T(8,128)(2,1)} fusion(bf16[8192,768]{1,0:T(8,128)(2,1)} %add_convert_fusion.8, bf16[8192,3072]{1,0:T(8,128)(2,1)} %fusion.199, bf16[4,768,3072]{2,1,0:T(8,128)(2,1)} %get-tuple-element.565, s32[]{:T(128)S(6)} %sub.35), kind=kOutput, calls=%fused_computation.70.clone.1 | convolution fusion | flops 38673580032 | bytes 80216064 | tf_op jit(solution)/shard_map/while/body/eval_jaxpr/tf,df->td/dot_general | solution.py:22
  1783.7 48.3 %bitcast_dynamic-update-slice_fusion.14 = f32[4,768,3072]{2,1,0:T(8,128)} fusion(f32[4,768,3072]{2,1,0:T(8,128)} %get-tuple-element.542, s32[]{:T(128)S(6)} %sub.35, bf16[8192,3072]{1,0:T(8,128)(2,1)} %fusion.199, bf16[4,8192,768]{2,1,0:T(8,128)(2,1)} %get-tuple-element.564), kind=kOutput, calls=%fused_computation.86.clone.1 | convolution fusion | flops 38654705664 | bytes 72352768 | tf_op jit(solution)/shard_map/while/body/eval_jaxpr/td,tf->df/dot_general | solution.py:21
  1874.9 27.5 fusion.197
  1937.2 50.4 %fusion.198 = f32[8192,3072]{1,0:T(8,128)} fusion(bf16[4,8192,768]{2,1,0:T(8,128)(2,1)} %get-tuple-element.564, s32[]{:T(128)S(6)} %sub.35, bf16[4,768,3072]{2,1,0:T(8,128)(2,1)} %get-tuple-element.565), kind=kOutput, calls=%fused_computation.74.clone.3 | convolution fusion | flops 38654705664 | bytes 117965824 | tf_op jit(solution)/shard_map/while/body/eval_jaxpr/dot_general | solution.py:15
  1987.6 56.9 %bitcast_dynamic-update-slice_fusion.15 = f32[4,3072,768]{2,1,0:T(8,128)} fusion(f32[4,3072,768]{2,1,0:T(8,128)} %get-tuple-element.543, s32[]{:T(128)S(6)} %sub.35, bf16[8192,768]{1,0:T(8,128)(2,1)} %add_convert_fusion.8, f32[8192,3072]{1,0:T(8,128)} %fusion.198), kind=kOutput, calls=%fused_computation.85.clone.2 | convolution fusion | flops 38881198080 | bytes 122683392 | tf_op jit(solution)/shard_map/while/body/eval_jaxpr/tf,td->fd/dot_general | solution.py:18
  2044.5 98.1 %fusion.199 = bf16[8192,3072]{1,0:T(8,128)(2,1)} fusion(f32[8192,3072]{1,0:T(8,128)} %fusion.198, bf16[8192,768]{1,0:T(8,128)(2,1)} %add_convert_fusion.8, bf16[4,3072,768]{2,1,0:T(8,128)(2,1)} %get-tuple-element.563, s32[]{:T(128)S(6)} %sub.35), kind=kOutput, calls=%fused_computation.52.clone.2 | convolution fusion | flops 39158022144 | bytes 168296448 | tf_op jit(solution)/shard_map/while/body/eval_jaxpr/td,fd->tf/dot_general | solution.py:19
  2142.6 47.6 %add_convert_fusion.9 = bf16[8192,768]{1,0:T(8,128)(2,1)} fusion(bf16[8192,768]{1,0:T(8,128)(2,1)} %add_convert_fusion.8, bf16[8192,3072]{1,0:T(8,128)(2,1)} %fusion.199, bf16[4,768,3072]{2,1,0:T(8,128)(2,1)} %get-tuple-element.565, s32[]{:T(128)S(6)} %sub.35), kind=kOutput, calls=%fused_computation.70.clone.1 | convolution fusion | flops 38673580032 | bytes 80216064 | tf_op jit(solution)/shard_map/while/body/eval_jaxpr/tf,df->td/dot_general | solution.py:22
  2190.2 48.2 %bitcast_dynamic-update-slice_fusion.14 = f32[4,768,3072]{2,1,0:T(8,128)} fusion(f32[4,768,3072]{2,1,0:T(8,128)} %get-tuple-element.542, s32[]{:T(128)S(6)} %sub.35, bf16[8192,3072]{1,0:T(8,128)(2,1)} %fusion.199, bf16[4,8192,768]{2,1,0:T(8,128)(2,1)} %get-tuple-element.564), kind=kOutput, calls=%fused_computation.86.clone.1 | convolution fusion | flops 38654705664 | bytes 72352768 | tf_op jit(solution)/shard_map/while/body/eval_jaxpr/td,tf->df/dot_general | solution.py:21
  2281.3 27.5 fusion.197
  2343.7 50.4 %fusion.198 = f32[8192,3072]{1,0:T(8,128)} fusion(bf16[4,8192,768]{2,1,0:T(8,128)(2,1)} %get-tuple-element.564, s32[]{:T(128)S(6)} %sub.35, bf16[4,768,3072]{2,1,0:T(8,128)(2,1)} %get-tuple-element.565), kind=kOutput, calls=%fused_computation.74.clone.3 | convolution fusion | flops 38654705664 | bytes 117965824 | tf_op jit(solution)/shard_map/while/body/eval_jaxpr/dot_general | solution.py:15
  2394.1 57.0 %bitcast_dynamic-update-slice_fusion.15 = f32[4,3072,768]{2,1,0:T(8,128)} fusion(f32[4,3072,768]{2,1,0:T(8,128)} %get-tuple-element.543, s32[]{:T(128)S(6)} %sub.35, bf16[8192,768]{1,0:T(8,128)(2,1)} %add_convert_fusion.8, f32[8192,3072]{1,0:T(8,128)} %fusion.198), kind=kOutput, calls=%fused_computation.85.clone.2 | convolution fusion | flops 38881198080 | bytes 122683392 | tf_op jit(solution)/shard_map/while/body/eval_jaxpr/tf,td->fd/dot_general | solution.py:18
  2451.1 98.4 %fusion.199 = bf16[8192,3072]{1,0:T(8,128)(2,1)} fusion(f32[8192,3072]{1,0:T(8,128)} %fusion.198, bf16[8192,768]{1,0:T(8,128)(2,1)} %add_convert_fusion.8, bf16[4,3072,768]{2,1,0:T(8,128)(2,1)} %get-tuple-element.563, s32[]{:T(128)S(6)} %sub.35), kind=kOutput, calls=%fused_computation.52.clone.2 | convolution fusion | flops 39158022144 | bytes 168296448 | tf_op jit(solution)/shard_map/while/body/eval_jaxpr/td,fd->tf/dot_general | solution.py:19
  2549.5 47.6 %add_convert_fusion.9 = bf16[8192,768]{1,0:T(8,128)(2,1)} fusion(bf16[8192,768]{1,0:T(8,128)(2,1)} %add_convert_fusion.8, bf16[8192,3072]{1,0:T(8,128)(2,1)} %fusion.199, bf16[4,768,3072]{2,1,0:T(8,128)(2,1)} %get-tuple-element.565, s32[]{:T(128)S(6)} %sub.35), kind=kOutput, calls=%fused_computation.70.clone.1 | convolution fusion | flops 38673580032 | bytes 80216064 | tf_op jit(solution)/shard_map/while/body/eval_jaxpr/tf,df->td/dot_general | solution.py:22
  2597.2 48.3 %bitcast_dynamic-update-slice_fusion.14 = f32[4,768,3072]{2,1,0:T(8,128)} fusion(f32[4,768,3072]{2,1,0:T(8,128)} %get-tuple-element.542, s32[]{:T(128)S(6)} %sub.35, bf16[8192,3072]{1,0:T(8,128)(2,1)} %fusion.199, bf16[4,8192,768]{2,1,0:T(8,128)(2,1)} %get-tuple-element.564), kind=kOutput, calls=%fused_computation.86.clone.1 | convolution fusion | flops 38654705664 | bytes 72352768 | tf_op jit(solution)/shard_map/while/body/eval_jaxpr/td,tf->df/dot_general | solution.py:21
  2648.8 69.7 %reduce-scatter.19.cloned.1.call-done = f32[1,768,768]{2,1,0:T(8,128)} async-done(((f32[4,768,768]{2,1,0:T(8,128)}), f32[1,768,768]{2,1,0:T(8,128)}) %reduce-scatter.19.cloned.1.call-update) | async-done | bytes 2359312
  2718.5 74.5 %reduce-scatter.17.cloned.1.call-done = f32[1,768,768]{2,1,0:T(8,128)} async-done(((f32[4,768,768]{2,1,0:T(8,128)}), f32[1,768,768]{2,1,0:T(8,128)}) %reduce-scatter.17.cloned.1.call-update) | async-done | bytes 2359312
  2793.0 254.4 %reduce-scatter.13.cloned.1.call-done = f32[1,768,3072]{2,1,0:T(8,128)} async-done(((f32[4,768,3072]{2,1,0:T(8,128)}), f32[1,768,3072]{2,1,0:T(8,128)}) %reduce-scatter.13.cloned.1.call-update) | async-done | bytes 9437200
  3047.4 254.4 %reduce-scatter.15.cloned.1.call-done = f32[1,3072,768]{2,1,0:T(8,128)} async-done(((f32[4,3072,768]{2,1,0:T(8,128)}), f32[1,3072,768]{2,1,0:T(8,128)}) %reduce-scatter.15.cloned.1.call-update) | async-done | bytes 9437200
  (52 shorter events, 358.0 us)
Async XLA Ops:
  7.2 55.4 %all-gather.9.cloned.1.call-start = ((), (), s32[]{:S(2)}) async-start(), calls=%async_computation.6 | async-start | bytes 5898240 | tf_op jit(solution)/shard_map/all_gather | solution.py:41
  7.2 13.0 copy-start
  25.0 73.6 %all-gather.11.cloned.1.call-start = ((), (), s32[]{:S(2)}) async-start(), calls=%async_computation.7 | async-start | bytes 5898240 | tf_op jit(solution)/shard_map/all_gather | solution.py:41
  25.8 192.5 %all-gather.5.cloned.1.call-start = ((), (), s32[]{:S(2)}) async-start(), calls=%async_computation.4 | async-start | bytes 23592960 | tf_op jit(solution)/shard_map/all_gather | solution.py:41
  26.5 311.2 %all-gather.7.cloned.1.call-start = ((), (), s32[]{:S(2)}) async-start(), calls=%async_computation.5 | async-start | bytes 23592960 | tf_op jit(solution)/shard_map/all_gather | solution.py:41
  27.1 2691.4 %reduce-scatter.19.cloned.1.call-start = ((), (), s32[]{:S(2)}) async-start(), calls=%async_computation.11 | async-start | bytes 11796480
  1036.9 24.7 copy-start.1
  1443.7 24.7 copy-start.1
  1850.3 24.7 copy-start.1
  2256.7 24.6 copy-start.1
  2646.7 146.3 %reduce-scatter.17.cloned.1.call-start = ((), (), s32[]{:S(2)}) async-start(), calls=%async_computation.10 | async-start | bytes 11796480
  2647.3 400.1 %reduce-scatter.13.cloned.1.call-start = ((), (), s32[]{:S(2)}) async-start(), calls=%async_computation.8 | async-start | bytes 47185920
  2648.0 653.8 %reduce-scatter.15.cloned.1.call-start = ((), (), s32[]{:S(2)}) async-start(), calls=%async_computation.9 | async-start | bytes 47185920
Sparse Core Ops, SparseCore 0:
  25.1 37.3 all-gather.8
  64.1 34.5 all-gather.10
  100.2 118.0 all-gather.4
  219.6 118.0 all-gather.6
  2646.8 71.6 reduce-scatter.18
  2721.5 71.5 reduce-scatter.16
  2796.2 251.2 reduce-scatter.12
  3050.6 251.2 reduce-scatter.14
where the time goes:
time: 3310 us
  matrix products  2220 us (67%)
  waiting for transfers between devices  967 us (29%)
  local copies, waits for them, and re-layouts  93.8 us (3%)
    unnamed x12, waiting for transfers between devices  657 us
    dot_general x8, matrix products, layer_backward(): jnp.einsum('td,fd->tf', grad_next, w_down, preferred_element_type=jnp.flo...  503 us
    dot_general x8, matrix products, layer_backward(): jnp.einsum('tf,td->fd', gelu_out, grad_next, preferred_element_type=jnp.f...  326 us
    dot_general x8, matrix products, layer_forward(): resid_delta = jnp.dot(gelu_out, w_down, preferred_element_type=jnp.float32)  319 us
    all_gather x4, waiting for transfers between devices, gather_round(): lax.all_gather(weight[round_idx], 'stage')  311 us
    dot_general x4, matrix products, layer_forward(): pre_act = jnp.dot(hidden, w_up, preferred_element_type=jnp.float32)  279 us
    dot_general x8, matrix products, layer_backward(): pre_act = jnp.dot(hidden, w_up, preferred_element_type=jnp.float32)  273 us
    dot_general x8, matrix products, layer_backward(): jnp.einsum('tf,df->td', d_pre, w_up, preferred_element_type=jnp.float32)  265 us
  transfers between devices with their start and end apart: 8, of which 8 were waited for; matrix products, arithmetic and copies ran while one was open for 0% of the time, Pallas kernels for 0%

commit v1 on v0

v1 whole, which is shorter than its diff:
```python
import functools

import jax
import jax.numpy as jnp
from jax import lax
from jax.experimental import pallas as pl
from jax.experimental.pallas import tpu as pltpu
from jax.sharding import PartitionSpec as P

BF = jnp.bfloat16
F32 = jnp.float32
SDS = jax.ShapeDtypeStruct
ANY = pl.BlockSpec(memory_space=pl.ANY)
C1 = 0.7978845608028654
C2 = C1 * 0.044715
CW = 768
VMEM_LIMIT = 63 * 2**20

SAME_CHIP = [(0, 1), (1, 0), (2, 3), (3, 2)]
CROSS_CHIP = [(0, 2), (1, 3), (2, 0), (3, 1)]


def dot_nn(a, b):
    return lax.dot_general(a, b, (((1,), (0,)), ((), ())), preferred_element_type=F32)


def dot_nt(a, b):
    return lax.dot_general(a, b, (((1,), (1,)), ((), ())), preferred_element_type=F32)


def gelu_gate(z):
    z2 = z * z
    return z2, 0.5 + 0.5 * jnp.tanh(z * (C1 + C2 * z2))


def gelu(z):
    return z * gelu_gate(z)[1]


def gelu_grad(z):
    z2, q = gelu_gate(z)
    return q + (z * (q * (1.0 - q))) * (2 * C1 + (6 * C2) * z2)


def load_weights(cands, bufs, sem):
    @pl.when(pl.program_id(0) == 0)
    def _():
        stage = lax.axis_index('stage')
        for k, cand in enumerate(cands):
            @pl.when(stage == k)
            def _(cand=cand):
                for i, (src, dst) in enumerate(zip(cand, bufs)):
                    pltpu.make_async_copy(src, dst, sem.at[i]).start()
        for i, (src, dst) in enumerate(zip(cands[0], bufs)):
            pltpu.make_async_copy(src, dst, sem.at[i]).wait()


def fwd_body(*refs, sub, save_a):
    h_ref, refs = refs[0], refs[2:]
    cands = [refs[4 * k:4 * k + 4] for k in range(4)]
    refs = refs[16:]
    za_ref, zb_ref, mid_ref, out_ref = refs[:4]
    refs = refs[4:]
    if save_a:
        aa_ref, ab_ref, refs = refs[0], refs[1], refs[2:]
    else:
        aa_ref, refs = refs[0], refs[1:]
    ua, wa, ub, wb, sem = refs
    load_weights(cands, (ua, wa, ub, wb), sem)
    rows, width = za_ref.shape
    for r in range(0, rows, sub):
        rs = slice(r, r + sub)
        h = h_ref[rs, :]
        for c in range(0, width, CW):
            cs = slice(c, c + CW)
            z = dot_nn(h, ua[:, cs])
            za_ref[rs, cs] = z
            aa_ref[rs, cs] = gelu(z).astype(BF)
        mid = (h.astype(F32) + dot_nn(aa_ref[rs, :], wa[...])).astype(BF)
        mid_ref[rs, :] = mid
        z = dot_nn(mid, ub[...])
        zb_ref[rs, :] = z
        a = gelu(z).astype(BF)
        if save_a:
            ab_ref[rs, :] = a
        out_ref[rs, :] = (mid.astype(F32) + dot_nn(a, wb[...])).astype(BF)


def weight_scratch(ws):
    return [pltpu.VMEM(w.shape, BF) for w in ws] + [pltpu.SemaphoreType.DMA((4,))]


def cost(flops, bytes_accessed):
    return pl.CostEstimate(flops=flops, bytes_accessed=bytes_accessed, transcendentals=0)


def fwd_pair(h, after, cands, save_a, rows=512, sub=256):
    n_tok, d = h.shape
    f, g = cands[0][0].shape[1], cands[0][2].shape[1]
    row = lambda n: pl.BlockSpec((rows, n), lambda i: (i, 0))
    outs = [(f, F32), (g, F32), (d, BF), (d, BF)] + ([(f, BF), (g, BF)] if save_a else [])
    scratch = ([] if save_a else [pltpu.VMEM((rows, f), BF)]) + weight_scratch(cands[0])
    return pl.pallas_call(
        functools.partial(fwd_body, sub=sub, save_a=save_a),
        grid=(n_tok // rows,),
        in_specs=[row(d)] + [ANY] * 17,
        out_specs=[row(n) for n, _ in outs],
        out_shape=[SDS((n_tok, n), t) for n, t in outs],
        scratch_shapes=scratch,
        cost_estimate=cost(4 * n_tok * d * (f + g), n_tok * (f + g) * 6),
        compiler_params=pltpu.CompilerParams(vmem_limit_bytes=VMEM_LIMIT),
        name='fwd_pair_a' if save_a else 'fwd_pair',
    )(h, after, *[w for cand in cands for w in cand])


def dgrad_body(*refs, sub, save_a):
    za_ref, zb_ref, g_ref, refs = refs[0], refs[1], refs[2], refs[4:]
    cands = [refs[4 * k:4 * k + 4] for k in range(4)]
    refs = refs[16:]
    dza_ref, dzb_ref, gm_ref, gp_ref = refs[:4]
    refs = refs[4:]
    if save_a:
        aa_ref, ab_ref, refs = refs[0], refs[1], refs[2:]
    ua, wa, ub, wb, sem = refs
    load_weights(cands, (ua, wa, ub, wb), sem)
    rows, width = za_ref.shape
    for r in range(0, rows, sub):
        rs = slice(r, r + sub)
        g = g_ref[rs, :]
        z = zb_ref[rs, :]
        if save_a:
            ab_ref[rs, :] = gelu(z).astype(BF)
        dz = (dot_nt(g, wb[...]) * gelu_grad(z)).astype(BF)
        dzb_ref[rs, :] = dz
        gm = (g.astype(F32) + dot_nt(dz, ub[...])).astype(BF)
        gm_ref[rs, :] = gm
        for c in range(0, width, CW):
            cs = slice(c, c + CW)
            z = za_ref[rs, cs]
            if save_a:
                aa_ref[rs, cs] = gelu(z).astype(BF)
            dza_ref[rs, cs] = (dot_nt(gm, wa[cs, :]) * gelu_grad(z)).astype(BF)
        gp_ref[rs, :] = (gm.astype(F32) + dot_nt(dza_ref[rs, :], ua[...])).astype(BF)


def dgrad_pair(za, zb, g, after, cands, save_a, rows=512, sub=256):
    n_tok, d = g.shape
    f, n = za.shape[1], zb.shape[1]
    row = lambda w: pl.BlockSpec((rows, w), lambda i: (i, 0))
    widths = [f, n, d, d] + ([f, n] if save_a else [])
    return pl.pallas_call(
        functools.partial(dgrad_body, sub=sub, save_a=save_a),
        grid=(n_tok // rows,),
        in_specs=[row(f), row(n), row(d)] + [ANY] * 17,
        out_specs=[row(w) for w in widths],
        out_shape=[SDS((n_tok, w), BF) for w in widths],
        scratch_shapes=weight_scratch(cands[0]),
        cost_estimate=cost(4 * n_tok * d * (f + n), n_tok * (f + n) * 6),
        compiler_params=pltpu.CompilerParams(vmem_limit_bytes=VMEM_LIMIT),
        name='dgrad_pair_a' if save_a else 'dgrad_pair',
    )(za, zb, g, after, *[w for cand in cands for w in cand])


def wgrad_body(*refs, ninit, phase, steps, rows, width):
    refs = refs[1:]
    cands = [refs[4 * k:4 * k + 4] for k in range(4)]
    refs = refs[16:]
    inits, out, refs = refs[:ninit], refs[ninit], refs[ninit + 1:]
    bufs, acc, refs = refs[:4], refs[4], refs[5:]
    if ninit:
        init_buf, refs = refs[0], refs[1:]
    sem, init_sem, out_sem = refs
    i = pl.program_id(0)
    stage = lax.axis_index('stage')
    kind = lax.rem(stage + phase, 2)
    sel = (stage // 2) * 2 + kind
    total = acc.shape[1]

    def tile_copies(step, slot, cand):
        rs = pl.ds(pl.multiple_of(step * rows, rows), rows)
        return [pltpu.make_async_copy(src.at[rs, :], dst.at[slot], sem.at[slot, k]) for k, (src, dst) in enumerate(zip(cand, bufs))]

    def start(step, slot):
        for k, cand in enumerate(cands):
            @pl.when(sel == k)
            def _(cand=cand):
                for cp in tile_copies(step, slot, cand):
                    cp.start()

    @pl.when(i == 0)
    def _():
        start(0, 0)
        for k in range(ninit):
            pltpu.make_async_copy(inits[k], init_buf.at[k], init_sem.at[k]).start()

    @pl.when(i + 1 < steps)
    def _():
        start(i + 1, (i + 1) % 2)

    slot = i % 2
    for cp in tile_copies(i, slot, cands[0]):
        cp.wait()
    xw, yw, xn, yn = [b.at[slot] for b in bufs]

    def product(mode):
        xt = xw[...].T
        for c in range(0, total, CW):
            cs = slice(c, c + CW)
            if c == width:
                xt = xn[...].T
            v = dot_nn(xt, yw[:, cs] if c < width else yn[:, c - width:c - width + CW])
            if mode == 'first':
                acc[:, cs] = v
            elif mode == 'mid':
                acc[:, cs] += v
            else:
                v = acc[:, cs] + v
                for k in range(ninit):
                    v = v + init_buf[k, :, cs]
                acc[:, cs] = v
                pltpu.make_async_copy(acc.at[:, cs], out.at[:, cs], out_sem.at[c // CW]).start()

    @pl.when(i == 0)
    def _():
        product('first')

    @pl.when((i > 0) & (i < steps - 1))
    def _():
        product('mid')

    @pl.when(i == steps - 1)
    def _():
        for k in range(ninit):
            pltpu.make_async_copy(inits[k], init_buf.at[k], init_sem.at[k]).wait()
        product('last')
        for c in range(0, total, CW):
            cs = slice(c, c + CW)
            pltpu.make_async_copy(acc.at[:, cs], out.at[:, cs], out_sem.at[c // CW]).wait()


def wgrad_half(after, pairs, phase, inits, rows=512):
    xw, yw, xn, yn = pairs[0][0]
    n_tok, d = xw.shape
    f, n = yw.shape[1], yn.shape[1]
    total = f + n
    scratch = [pltpu.VMEM((2, rows, w), BF) for w in (d, f, d, n)] + [pltpu.VMEM((d, total), F32)]
    if inits:
        scratch.append(pltpu.VMEM((len(inits), d, total), F32))
    scratch += [pltpu.SemaphoreType.DMA((2, 4)), pltpu.SemaphoreType.DMA((max(1, len(inits)),)), pltpu.SemaphoreType.DMA((total // CW,))]
    flat = [r for pair in pairs for cand in pair for r in cand]
    return pl.pallas_call(
        functools.partial(wgrad_body, ninit=len(inits), phase=phase, steps=n_tok // rows, rows=rows, width=f),
        grid=(n_tok // rows,),
        in_specs=[ANY] * (1 + len(flat) + len(inits)),
        out_specs=ANY,
        out_shape=SDS((d, total), F32),
        scratch_shapes=scratch,
        cost_estimate=cost(2 * n_tok * d * total, n_tok * total * 2),
        compiler_params=pltpu.CompilerParams(vmem_limit_bytes=VMEM_LIMIT),
        name=f'wgrad_{phase}_{len(inits)}',
    )(after, *flat, *inits)


def solution(mesh):
    tok_spec = P(('data', 'stage'))
    row_spec = P('stage')

    def device_body(acts_in, grad_out, w_up_a, w_down_a, w_up_b, w_down_b):
        n_micro, tokens, d = acts_in.shape
        n_tok = n_micro * tokens
        perm = lambda xs, pairs: tuple(lax.ppermute(x, 'stage', pairs) for x in xs)
        own = tuple(w[0] for w in (w_up_a, w_down_a, w_up_b, w_down_b))
        f = own[0].shape[1]

        peer = perm(own, SAME_CHIP)
        cross_even = perm(own, [(0, 2), (2, 0)])
        own_late, cross_even = lax.optimization_barrier((own, cross_even))
        far_odd = perm(cross_even, [(2, 3), (0, 1)])
        cross_odd = perm(own_late, [(1, 3), (3, 1)])
        far_even = perm(cross_odd, [(3, 2), (1, 0)])
        cands = [
            [own, peer, cross_even, far_odd],
            [peer, own, far_even, cross_odd],
            [cross_even, far_odd, own, peer],
            [far_even, cross_odd, peer, own],
        ]
        save_a = [True, True, False, False]

        h = acts_in.reshape(n_tok, d)
        saved = []
        after = h
        for j in range(4):
            outs = fwd_pair(h, after, cands[j], save_a[j])
            za, zb, mid, nxt = outs[:4]
            saved.append([h, mid, za, zb, *outs[4:]])
            h = after = nxt
        acts_out = h

        up_ops, down_ops = {}, {}
        g = grad_out.reshape(n_tok, d)

        def dgrad(j, g, after):
            h, mid, za, zb, *acts = saved[j]
            outs = dgrad_pair(za, zb, g, after, cands[j], not save_a[j])
            dza, dzb, gm, gp = outs[:4]
            aa, ab = acts if save_a[j] else outs[4:]
            up_ops[j] = (h, dza, mid, dzb)
            down_ops[j] = (gm, aa, g, ab)
            return gp

        def wgrad(after, pair0, pair1, phase, inits=()):
            pairs = [(up_ops[p], down_ops[p]) for p in (pair0, pair1)]
            return wgrad_half(after, pairs, phase, list(inits))

        swap = lambda x: lax.ppermute(x, 'stage', SAME_CHIP)
        cross = lambda x: lax.ppermute(x, 'stage', CROSS_CHIP)

        g = dgrad(3, g, after)
        g = dgrad(2, g, g)
        g = dgrad(1, g, g)
        a1 = wgrad(g, 3, 1, 0)
        a2 = wgrad(a1, 3, 1, 1, [swap(a1)])
        a_in = cross(a2)
        g = dgrad(0, g, a2)
        b1 = wgrad(g, 2, 0, 0)
        b2 = wgrad(b1, 2, 0, 1, [swap(b1)])
        b_in = cross(b2)
        c1 = wgrad(b2, 1, 3, 0)
        d1 = wgrad(c1, 0, 2, 0)
        c2 = wgrad(d1, 1, 3, 1, [swap(c1), a_in])
        d2 = wgrad(c2, 0, 2, 1, [swap(d1), b_in])
        c_in = lax.ppermute(c2, 'stage', [(0, 1), (2, 3)])
        d_in = lax.ppermute(d2, 'stage', [(1, 0), (3, 2)])
        odd = lax.axis_index('stage') % 2 == 1
        up = jnp.where(odd, c2, d_in)
        down = jnp.where(odd, c_in, d2)
        return (
            acts_out.reshape(acts_in.shape),
            g.reshape(acts_in.shape),
            up[None, :, :f],
            down[:, :f].T[None],
            up[None, :, f:],
            down[:, f:].T[None],
        )

    return jax.shard_map(device_body, mesh=mesh, in_specs=(tok_spec, tok_spec, row_spec, row_spec, row_spec, row_spec), out_specs=(tok_spec,) * 6, check_vma=False)
```

time: 3310 us -> 2230 us (0.67)
  matrix products: 2220 us -> 0 us
  Pallas kernels: 0 us -> 1590 us
  waiting for transfers between devices: 967 us -> 403 us
  starting transfers between devices: 0.31 us -> 171 us
  local copies, waits for them, and re-layouts: 93.8 us -> 39.2 us
    dot_general x52 -> x0, matrix products: 2220 us -> none  [the longest x8 503 us: layer_backward(): jnp.einsum('td,fd->tf', grad_next, w_down, preferred_element_type=jnp.flo...]
    pallas_call x0 -> x16, Pallas kernels: none -> 1590 us  [the longest x4 576 us: dgrad_pair(): pl.pallas_call(functools.partial(dgrad_body, sub=sub, save_a=save_a), gri...]
    unnamed x12 -> x0, waiting for transfers between devices: 657 us -> none
    ppermute x0 -> x28, waiting for transfers between devices: none -> 403 us  [the longest x2 238 us: device_body(): cross = lambda x: lax.ppermute(x, 'stage', CROSS_CHIP)]
    all_gather x4 -> x0, waiting for transfers between devices: 311 us -> none  [gather_round(): lax.all_gather(weight[round_idx], 'stage')]
    ppermute x0 -> x28, starting transfers between devices: none -> 171 us  [the longest x4 122 us: device_body(): swap = lambda x: lax.ppermute(x, 'stage', SAME_CHIP)]
    dynamic_update_slice x4 -> x0, local copies, waits for them, and re-layouts: 42.2 us -> none  [device_body(): lax.scan(pair_forward, hidden, gather_round(local_rows, round_idx))]
  transfers between devices with their start and end apart: 8 -> 28, of which waited for: 8 -> 8; matrix products, arithmetic and copies ran while one was open for 0% -> 1% of each run, Pallas kernels for 0% -> 20%
where the time goes in v1:
time: 2230 us; the launch traced here: 2220 us
  Pallas kernels  1590 us (71%)
  waiting for transfers between devices  403 us (18%)
  starting transfers between devices  171 us (8%)
  local copies, waits for them, and re-layouts  39.2 us (2%)
    pallas_call x4, Pallas kernels, dgrad_pair(): pl.pallas_call(functools.partial(dgrad_body, sub=sub, save_a=save_a), gri...  576 us
    pallas_call x4, Pallas kernels, fwd_pair(): pl.pallas_call(functools.partial(fwd_body, sub=sub, save_a=save_a), grid=...  524 us
    pallas_call x8, Pallas kernels, wgrad_half(): pl.pallas_call(functools.partial(wgrad_body, ninit=len(inits), phase=phas...  489 us
    ppermute x2, waiting for transfers between devices, device_body(): cross = lambda x: lax.ppermute(x, 'stage', CROSS_CHIP)  238 us
    ppermute x20, waiting for transfers between devices, device_body(): lax.ppermute(x, 'stage', pairs)  131 us
    ppermute x4, starting transfers between devices, device_body(): swap = lambda x: lax.ppermute(x, 'stage', SAME_CHIP)  122 us
  transfers between devices with their start and end apart: 28, of which 8 were waited for; matrix products, arithmetic and copies ran while one was open for 1% of the time, Pallas kernels for 20%

profile of v1, /device:TPU:0, one launch (start us, length us, event | category | flops | bytes accessed | tf_op | source)
XLA Modules:
  0.0 2219.2 jit_solution(18013046827931038478)
XLA Ops:
  0.6 5.3 collective-permute-start.4
  5.9 1.9 collective-permute-start.5
  8.4 3.9 collective-permute-start.6
  12.3 108.9 %collective-permute-done.6.refs_12_.refs_4_.refs_6_.refs_14_ = bf16[768,768]{1,0:T(8,128)(2,1)S(1)} collective-permute-done((bf16[768,768]{1,0:T(8,128)(2,1)}, bf16[768,768]{1,0:T(8,128)(2,1)S(1)}, u32[]{:S(2)}, u32[]{:S(2)}) %collective-permute-start.6) | collective-permute-done | bytes 1179680 | tf_op jit(solution)/shard_map/ppermute | solution.py:271
  121.2 3.9 collective-permute-start.7
  125.1 14.2 collective-permute-done.7.refs_13_.refs_5_.refs_7_.refs_15_
  139.8 2.0 collective-permute-start.10
  142.1 2.4 collective-permute-start.8
  144.5 2.8 collective-permute-start.12
  147.3 3.2 collective-permute-start.14
  150.6 1.6 collective-permute-start.9
  152.2 1.4 collective-permute-start.11
  153.5 7.5 collective-permute-done.11.refs_17_.refs_9_.refs_11_.refs_19_
  161.1 1.7 collective-permute-start.16
  162.7 1.7 collective-permute-start.18
  169.8 2.1 copy-done.6
  171.9 131.6 %fwd_pair_a.2 = (f32[8192,3072]{1,0:T(8,128)}, f32[8192,768]{1,0:T(8,128)}, bf16[8192,768]{1,0:T(8,128)(2,1)}, bf16[8192,768]{1,0:T(8,128)(2,1)}, bf16[8192,3072]{1,0:T(8,128)(2,1)}, /*index=5*/bf16[8192,768]{1,0:T(8,128)(2,1)}) custom-call(bf16[8192,768]{1,0:T(8,128)(2,1)} %bitcast.25, bf16[8192,768]{1,0:T(8,128)(2,1)} %bitcast.26, ...), custom_call_target="tpu_custom_call" | custom-call | flops 96636764160 | bytes 188743680 | tf_op jit(solution)/shard_map/fwd_pair_a/pallas_call | solution.py:103
  303.5 131.9 %fwd_pair_a.3 = (f32[8192,3072]{1,0:T(8,128)}, f32[8192,768]{1,0:T(8,128)}, bf16[8192,768]{1,0:T(8,128)(2,1)}, bf16[8192,768]{1,0:T(8,128)(2,1)}, bf16[8192,3072]{1,0:T(8,128)(2,1)}, /*index=5*/bf16[8192,768]{1,0:T(8,128)(2,1)}) custom-call(bf16[8192,768]{1,0:T(8,128)(2,1)} %get-tuple-element.58.refs_0_.refs_1_.refs_9_, ...), custom_call_target="tpu_custom_call" | custom-call | flops 96636764160 | bytes 188743680 | tf_op jit(solution)/shard_map/fwd_pair_a/pallas_call | solution.py:103
  435.5 130.2 %fwd_pair.2 = (f32[8192,3072]{1,0:T(8,128)}, f32[8192,768]{1,0:T(8,128)}, bf16[8192,768]{1,0:T(8,128)(2,1)}, bf16[8192,768]{1,0:T(8,128)(2,1)}) custom-call(bf16[8192,768]{1,0:T(8,128)(2,1)} %get-tuple-element.63.refs_0_.refs_1_.refs_9_, bf16[8192,768]{1,0:T(8,128)(2,1)} %get-tuple-element.63.refs_0_.refs_1_.refs_9_, bf16[768,3072]{1,0:T(8,128)(2,1)} %copy-done.1, ...), custom_call_target="tpu_custom_call" | custom-call | flops 96636764160 | bytes 188743680 | tf_op jit(solution)/shard_map/fwd_pair/pallas_call | solution.py:103
  565.7 130.5 %fwd_pair.3 = (f32[8192,3072]{1,0:T(8,128)}, f32[8192,768]{1,0:T(8,128)}, bf16[8192,768]{1,0:T(8,128)(2,1)}, bf16[8192,768]{1,0:T(8,128)(2,1)}) custom-call(bf16[8192,768]{1,0:T(8,128)(2,1)} %get-tuple-element.64.refs_0_.refs_1_.refs_9_, bf16[8192,768]{1,0:T(8,128)(2,1)} %get-tuple-element.64.refs_0_.refs_1_.refs_9_, ...), custom_call_target="tpu_custom_call" | custom-call | flops 96636764160 | bytes 188743680 | tf_op jit(solution)/shard_map/fwd_pair/pallas_call | solution.py:103
  696.2 148.4 %dgrad_pair_a.2 = (bf16[8192,3072]{1,0:T(8,128)(2,1)}, bf16[8192,768]{1,0:T(8,128)(2,1)}, bf16[8192,768]{1,0:T(8,128)(2,1)}, bf16[8192,768]{1,0:T(8,128)(2,1)}, ...) custom-call(f32[8192,3072]{1,0:T(8,128)} %get-tuple-element.72.refs_0_, f32[8192,768]{1,0:T(8,128)} %get-tuple-element.73.refs_1_, ...), custom_call_target="tpu_custom_call" | custom-call | flops 96636764160 | bytes 188743680 | tf_op jit(solution)/shard_map/dgrad_pair_a/pallas_call | solution.py:151
  844.6 148.4 %dgrad_pair_a.3 = (bf16[8192,3072]{1,0:T(8,128)(2,1)}, bf16[8192,768]{1,0:T(8,128)(2,1)}, bf16[8192,768]{1,0:T(8,128)(2,1)}, bf16[8192,768]{1,0:T(8,128)(2,1)}, ...) custom-call(f32[8192,3072]{1,0:T(8,128)} %get-tuple-element.70.refs_0_, f32[8192,768]{1,0:T(8,128)} %get-tuple-element.71.refs_1_, ...), custom_call_target="tpu_custom_call" | custom-call | flops 96636764160 | bytes 188743680 | tf_op jit(solution)/shard_map/dgrad_pair_a/pallas_call | solution.py:151
  993.0 139.8 %dgrad_pair.2 = (bf16[8192,3072]{1,0:T(8,128)(2,1)}, bf16[8192,768]{1,0:T(8,128)(2,1)}, bf16[8192,768]{1,0:T(8,128)(2,1)}, bf16[8192,768]{1,0:T(8,128)(2,1)}) custom-call(f32[8192,3072]{1,0:T(8,128)} %get-tuple-element.68.refs_0_, f32[8192,768]{1,0:T(8,128)} %get-tuple-element.69.refs_1_, ...), custom_call_target="tpu_custom_call" | custom-call | flops 96636764160 | bytes 188743680 | tf_op jit(solution)/shard_map/dgrad_pair/pallas_call | solution.py:151
  1132.8 58.7 %wgrad_0_0.4.refs_0_ = f32[768,3840]{1,0:T(8,128)} custom-call(bf16[8192,768]{1,0:T(8,128)(2,1)} %get-tuple-element.76.refs_0_.refs_2_.refs_15_.refs_7_, bf16[8192,768]{1,0:T(8,128)(2,1)} %get-tuple-element.64.refs_0_.refs_1_.refs_9_, bf16[8192,3072]{1,0:T(8,128)(2,1)} %get-tuple-element.77.refs_2_.refs_10_, ...), custom_call_target="tpu_custom_call" | custom-call | flops 48318382080 | bytes 62914560 | tf_op jit(solution)/shard_map/wgrad_0_0/pallas_call | solution.py:251
  1191.5 121.5 %collective-permute-start.20 = (f32[768,3840]{1,0:T(8,128)}, f32[768,3840]{1,0:T(8,128)}, u32[]{:S(2)}, u32[]{:S(2)}) collective-permute-start(f32[768,3840]{1,0:T(8,128)} %wgrad_0_0.4.refs_0_), channel_id=1, source_target_pairs={{0,1},{1,0},{2,3},{3,2},{4,5},{5,4},{6,7},{7,6}} | collective-permute-start | bytes 35389448 | tf_op jit(solution)/shard_map/ppermute | solution.py:315
  1313.0 17.7 collective-permute-done.20.refs_17_
  1330.7 61.8 %wgrad_1_1.2.refs_3_ = f32[768,3840]{1,0:T(8,128)} custom-call(f32[768,3840]{1,0:T(8,128)} %wgrad_0_0.4.refs_0_, bf16[8192,768]{1,0:T(8,128)(2,1)} %get-tuple-element.64.refs_0_.refs_1_.refs_9_, bf16[8192,3072]{1,0:T(8,128)(2,1)} %get-tuple-element.77.refs_2_.refs_10_, bf16[8192,768]{1,0:T(8,128)(2,1)} %get-tuple-element.78.refs_3_.refs_11_, ...), custom_call_target="tpu_custom_call" | custom-call | flops 48318382080 | bytes 62914560 | tf_op jit(solution)/shard_map/wgrad_1_1/pallas_call | solution.py:251
  1392.5 139.8 %dgrad_pair.3 = (bf16[8192,3072]{1,0:T(8,128)(2,1)}, bf16[8192,768]{1,0:T(8,128)(2,1)}, bf16[8192,768]{1,0:T(8,128)(2,1)}, bf16[8192,768]{1,0:T(8,128)(2,1)}) custom-call(f32[8192,3072]{1,0:T(8,128)} %get-tuple-element.66.refs_0_, f32[8192,768]{1,0:T(8,128)} %get-tuple-element.67.refs_1_, ...), custom_call_target="tpu_custom_call" | custom-call | flops 96636764160 | bytes 188743680 | tf_op jit(solution)/shard_map/dgrad_pair/pallas_call | solution.py:151
  1532.2 58.5 %wgrad_0_0.5.refs_0_ = f32[768,3840]{1,0:T(8,128)} custom-call(bf16[8192,768]{1,0:T(8,128)(2,1)} %get-tuple-element.89.refs_0_, bf16[8192,768]{1,0:T(8,128)(2,1)} %get-tuple-element.63.refs_0_.refs_1_.refs_9_, bf16[8192,3072]{1,0:T(8,128)(2,1)} %get-tuple-element.90.refs_2_.refs_10_, bf16[8192,768]{1,0:T(8,128)(2,1)} %get-tuple-element.91.refs_3_.refs_11_, ...), custom_call_target="tpu_custom_call" | custom-call | flops 48318382080 | bytes 62914560 | tf_op jit(solution)/shard_map/wgrad_0_0/pallas_call | solution.py:251
  1591.1 1.7 collective-permute-start.23
  1592.8 16.0 collective-permute-done.21.refs_17_
  1608.8 62.2 %wgrad_1_1.3.refs_0_ = f32[768,3840]{1,0:T(8,128)} custom-call(f32[768,3840]{1,0:T(8,128)} %wgrad_0_0.5.refs_0_, bf16[8192,768]{1,0:T(8,128)(2,1)} %get-tuple-element.63.refs_0_.refs_1_.refs_9_, bf16[8192,3072]{1,0:T(8,128)(2,1)} %get-tuple-element.90.refs_2_.refs_10_, bf16[8192,768]{1,0:T(8,128)(2,1)} %get-tuple-element.91.refs_3_.refs_11_, ...), custom_call_target="tpu_custom_call" | custom-call | flops 48318382080 | bytes 62914560 | tf_op jit(solution)/shard_map/wgrad_1_1/pallas_call | solution.py:251
  1671.0 58.4 %wgrad_0_0.6.refs_0_ = f32[768,3840]{1,0:T(8,128)} custom-call(f32[768,3840]{1,0:T(8,128)} %wgrad_1_1.3.refs_0_, bf16[8192,768]{1,0:T(8,128)(2,1)} %get-tuple-element.58.refs_0_.refs_1_.refs_9_, bf16[8192,3072]{1,0:T(8,128)(2,1)} %get-tuple-element.83.refs_10_.refs_2_, bf16[8192,768]{1,0:T(8,128)(2,1)} %get-tuple-element.84.refs_11_.refs_3_, ...), custom_call_target="tpu_custom_call" | custom-call | flops 48318382080 | bytes 62914560 | tf_op jit(solution)/shard_map/wgrad_0_0/pallas_call | solution.py:251
  1729.7 58.5 %wgrad_0_0.7.refs_0_ = f32[768,3840]{1,0:T(8,128)} custom-call(f32[768,3840]{1,0:T(8,128)} %wgrad_0_0.6.refs_0_, bf16[8192,768]{1,0:T(8,128)(2,1)} %bitcast.29, bf16[8192,3072]{1,0:T(8,128)(2,1)} %get-tuple-element.96.refs_10_.refs_2_, bf16[8192,768]{1,0:T(8,128)(2,1)} %get-tuple-element.97.refs_11_.refs_3_, ...), custom_call_target="tpu_custom_call" | custom-call | flops 48318382080 | bytes 62914560 | tf_op jit(solution)/shard_map/wgrad_0_0/pallas_call | solution.py:251
  1788.5 1.6 collective-permute-start.25
  1790.1 57.4 %collective-permute-done.23.refs_18_ = f32[768,3840]{1,0:T(8,128)} collective-permute-done((f32[768,3840]{1,0:T(8,128)}, f32[768,3840]{1,0:T(8,128)}, u32[]{:S(2)}, u32[]{:S(2)}) %collective-permute-start.23) | collective-permute-done | bytes 11796512 | tf_op jit(solution)/shard_map/ppermute | solution.py:316
  1847.5 65.4 %wgrad_1_2.2.refs_0_ = f32[768,3840]{1,0:T(8,128)} custom-call(f32[768,3840]{1,0:T(8,128)} %wgrad_0_0.7.refs_0_, bf16[8192,768]{1,0:T(8,128)(2,1)} %get-tuple-element.58.refs_0_.refs_1_.refs_9_, bf16[8192,3072]{1,0:T(8,128)(2,1)} %get-tuple-element.83.refs_10_.refs_2_, bf16[8192,768]{1,0:T(8,128)(2,1)} %get-tuple-element.84.refs_11_.refs_3_, ...), custom_call_target="tpu_custom_call" | custom-call | flops 48318382080 | bytes 62914560 | tf_op jit(solution)/shard_map/wgrad_1_2/pallas_call | solution.py:251
  1912.9 5.6 collective-permute-start.27
  1918.5 181.0 %collective-permute-done.25.refs_18_ = f32[768,3840]{1,0:T(8,128)} collective-permute-done((f32[768,3840]{1,0:T(8,128)}, f32[768,3840]{1,0:T(8,128)}, u32[]{:S(2)}, u32[]{:S(2)}) %collective-permute-start.25) | collective-permute-done | bytes 11796512 | tf_op jit(solution)/shard_map/ppermute | solution.py:316
  2099.5 65.6 %wgrad_1_2.3 = f32[768,3840]{1,0:T(8,128)} custom-call(f32[768,3840]{1,0:T(8,128)} %wgrad_1_2.2.refs_0_, bf16[8192,768]{1,0:T(8,128)(2,1)} %bitcast.30, bf16[8192,3072]{1,0:T(8,128)(2,1)} %get-tuple-element.96.refs_10_.refs_2_, bf16[8192,768]{1,0:T(8,128)(2,1)} %get-tuple-element.97.refs_11_.refs_3_, bf16[8192,768]{1,0:T(8,128)(2,1)} %get-tuple-element.98.refs_12_.refs_4_, ...), custom_call_target="tpu_custom_call" | custom-call | flops 48318382080 | bytes 62914560 | tf_op jit(solution)/shard_map/wgrad_1_2/pallas_call | solution.py:251
  2166.5 5.5 broadcast_select_fusion
  2172.0 4.3 copy-done
  2176.4 9.2 slice_bitcast_fusion
  2185.7 10.0 broadcast_select_fusion.1
  2195.7 8.6 slice_bitcast_fusion.1
  2204.3 3.2 slice_bitcast_fusion.3
  2207.5 9.6 copy.12
  2217.1 1.9 copy.13
  (63 shorter events, 8.9 us)
Async XLA Ops:
  0.6 138.6 %collective-permute-start.4 = (bf16[768,3072]{1,0:T(8,128)(2,1)}, bf16[768,3072]{1,0:T(8,128)(2,1)S(1)}, u32[]{:S(2)}, u32[]{:S(2)}) collective-permute-start(bf16[768,3072]{1,0:T(8,128)(2,1)} %bitcast.34), channel_id=1, source_target_pairs={{0,2},{2,0},{4,6},{6,4}} | collective-permute-start | bytes 14155784 | tf_op jit(solution)/shard_map/ppermute | solution.py:271
  5.9 133.9 %collective-permute-start.5 = (bf16[3072,768]{1,0:T(8,128)(2,1)}, bf16[3072,768]{1,0:T(8,128)(2,1)S(1)}, u32[]{:S(2)}, u32[]{:S(2)}) collective-permute-start(bf16[3072,768]{1,0:T(8,128)(2,1)} %bitcast.45), channel_id=1, source_target_pairs={{0,2},{2,0},{4,6},{6,4}} | collective-permute-start | bytes 14155784 | tf_op jit(solution)/shard_map/ppermute | solution.py:271
  7.8 139.5 %collective-permute-start = (bf16[768,3072]{1,0:T(8,128)(2,1)}, bf16[768,3072]{1,0:T(8,128)(2,1)S(1)}, u32[]{:S(2)}, u32[]{:S(2)}) collective-permute-start(bf16[768,3072]{1,0:T(8,128)(2,1)} %bitcast.35), channel_id=1, source_target_pairs={{0,1},{1,0},{2,3},{3,2},{4,5},{5,4},{6,7},{7,6}} | collective-permute-start | bytes 14155784 | tf_op jit(solution)/shard_map/ppermute | solution.py:271
  7.9 142.7 %collective-permute-start.1 = (bf16[3072,768]{1,0:T(8,128)(2,1)}, bf16[3072,768]{1,0:T(8,128)(2,1)S(1)}, u32[]{:S(2)}, u32[]{:S(2)}) collective-permute-start(bf16[3072,768]{1,0:T(8,128)(2,1)} %bitcast.46), channel_id=1, source_target_pairs={{0,1},{1,0},{2,3},{3,2},{4,5},{5,4},{6,7},{7,6}} | collective-permute-start | bytes 14155784 | tf_op jit(solution)/shard_map/ppermute | solution.py:271
  8.4 112.8 %collective-permute-start.6 = (bf16[768,768]{1,0:T(8,128)(2,1)}, bf16[768,768]{1,0:T(8,128)(2,1)S(1)}, u32[]{:S(2)}, u32[]{:S(2)}) collective-permute-start(bf16[768,768]{1,0:T(8,128)(2,1)} %bitcast.56), channel_id=1, source_target_pairs={{0,2},{2,0},{4,6},{6,4}} | collective-permute-start | bytes 3538952 | tf_op jit(solution)/shard_map/ppermute | solution.py:271
  121.2 48.5 %copy-start.7 = (bf16[768,768]{1,0:T(8,128)(2,1)}, bf16[768,768]{1,0:T(8,128)(2,1)S(1)}, u32[]{:S(2)}) copy-start(bf16[768,768]{1,0:T(8,128)(2,1)S(1)} %collective-permute-done.6.refs_12_.refs_4_.refs_6_.refs_14_) | copy-start | bytes 3538948
  121.2 18.1 collective-permute-start.7
  139.3 30.4 %copy-start.8 = (bf16[768,768]{1,0:T(8,128)(2,1)}, bf16[768,768]{1,0:T(8,128)(2,1)S(1)}, u32[]{:S(2)}) copy-start(bf16[768,768]{1,0:T(8,128)(2,1)S(1)} %collective-permute-done.7.refs_13_.refs_5_.refs_7_.refs_15_) | copy-start | bytes 3538948
  139.3 2.8 collective-permute-start.2
  139.3 2.8 copy-start.1
  139.3 5.2 collective-permute-start.3
  139.8 26.0 %copy-start.2 = (bf16[3072,768]{1,0:T(8,128)(2,1)}, bf16[3072,768]{1,0:T(8,128)(2,1)S(1)}, u32[]{:S(2)}) copy-start(bf16[3072,768]{1,0:T(8,128)(2,1)S(1)} %collective-permute-done.5.refs_11_.refs_3_.refs_5_.refs_13_) | copy-start | bytes 14155780
  139.8 12.4 collective-permute-start.10
  142.1 23.7 %collective-permute-start.8 = (bf16[768,3072]{1,0:T(8,128)(2,1)S(1)}, bf16[768,3072]{1,0:T(8,128)(2,1)S(1)}, u32[]{:S(2)}, u32[]{:S(2)}) collective-permute-start(bf16[768,3072]{1,0:T(8,128)(2,1)S(1)} %collective-permute-done.4.refs_10_.refs_2_.refs_4_.refs_12_), channel_id=1, source_target_pairs={{2,3},{0,1},{6,7},{4,5}} | collective-permute-start | bytes 14155784 | tf_op jit(solution)/shard_map/ppermute | solution.py:271
  144.5 6.1 copy-start.9
  144.5 22.6 %collective-permute-start.12 = (bf16[768,3072]{1,0:T(8,128)(2,1)}, bf16[768,3072]{1,0:T(8,128)(2,1)}, u32[]{:S(2)}, u32[]{:S(2)}) collective-permute-start(bf16[768,3072]{1,0:T(8,128)(2,1)} %bitcast.36), channel_id=1, source_target_pairs={{1,3},{3,1},{5,7},{7,5}} | collective-permute-start | bytes 14155784 | tf_op jit(solution)/shard_map/ppermute | solution.py:271
  147.3 22.4 %copy-start.3 = (bf16[768,3072]{1,0:T(8,128)(2,1)}, bf16[768,3072]{1,0:T(8,128)(2,1)S(1)}, u32[]{:S(2)}) copy-start(bf16[768,3072]{1,0:T(8,128)(2,1)S(1)} %collective-permute-done.refs_6_.refs_2_.refs_14_.refs_10_.refs_12_.refs_16_.refs_4_.refs_8_) | copy-start | bytes 14155780
  147.3 21.1 collective-permute-start.14
  150.6 19.2 copy-start.4
  150.6 19.1 collective-permute-start.9
  152.2 17.6 copy-start.10
  152.2 8.9 collective-permute-start.11
  161.1 8.7 copy-start.11
  161.1 1.7 collective-permute-start.16
  162.7 1.7 collective-permute-start.18
  164.4 139.1 %collective-permute-start.17 = (bf16[768,768]{1,0:T(8,128)(2,1)}, bf16[768,768]{1,0:T(8,128)(2,1)}, u32[]{:S(2)}, u32[]{:S(2)}) collective-permute-start(bf16[768,768]{1,0:T(8,128)(2,1)} %collective-permute-done.16.refs_16_.refs_8_.refs_10_.refs_18_), channel_id=1, source_target_pairs={{3,2},{1,0},{7,6},{5,4}} | collective-permute-start | bytes 3538952 | tf_op jit(solution)/shard_map/ppermute | solution.py:271
  165.8 4.0 copy-start.5
  165.8 137.8 %collective-permute-start.19 = (bf16[768,768]{1,0:T(8,128)(2,1)}, bf16[768,768]{1,0:T(8,128)(2,1)}, u32[]{:S(2)}, u32[]{:S(2)}) collective-permute-start(bf16[768,768]{1,0:T(8,128)(2,1)} %collective-permute-done.18.refs_17_.refs_9_.refs_11_.refs_19_), channel_id=1, source_target_pairs={{3,2},{1,0},{7,6},{5,4}} | collective-permute-start | bytes 3538952 | tf_op jit(solution)/shard_map/ppermute | solution.py:271
  167.1 136.5 %collective-permute-start.13 = (bf16[768,3072]{1,0:T(8,128)(2,1)}, bf16[768,3072]{1,0:T(8,128)(2,1)}, u32[]{:S(2)}, u32[]{:S(2)}) collective-permute-start(bf16[768,3072]{1,0:T(8,128)(2,1)} %collective-permute-done.12.refs_14_.refs_6_.refs_8_.refs_16_), channel_id=1, source_target_pairs={{3,2},{1,0},{7,6},{5,4}} | collective-permute-start | bytes 14155784 | tf_op jit(solution)/shard_map/ppermute | solution.py:271
  168.4 135.2 %collective-permute-start.15 = (bf16[3072,768]{1,0:T(8,128)(2,1)}, bf16[3072,768]{1,0:T(8,128)(2,1)}, u32[]{:S(2)}, u32[]{:S(2)}) collective-permute-start(bf16[3072,768]{1,0:T(8,128)(2,1)} %collective-permute-done.14.refs_15_.refs_7_.refs_9_.refs_17_), channel_id=1, source_target_pairs={{3,2},{1,0},{7,6},{5,4}} | collective-permute-start | bytes 14155784 | tf_op jit(solution)/shard_map/ppermute | solution.py:271
  169.8 2.2 copy-start.6
  1191.5 139.1 %collective-permute-start.20 = (f32[768,3840]{1,0:T(8,128)}, f32[768,3840]{1,0:T(8,128)}, u32[]{:S(2)}, u32[]{:S(2)}) collective-permute-start(f32[768,3840]{1,0:T(8,128)} %wgrad_0_0.4.refs_0_), channel_id=1, source_target_pairs={{0,1},{1,0},{2,3},{3,2},{4,5},{5,4},{6,7},{7,6}} | collective-permute-start | bytes 35389448 | tf_op jit(solution)/shard_map/ppermute | solution.py:315
  1590.8 18.0 collective-permute-start.21
  1591.1 256.4 %collective-permute-start.23 = (f32[768,3840]{1,0:T(8,128)}, f32[768,3840]{1,0:T(8,128)}, u32[]{:S(2)}, u32[]{:S(2)}) collective-permute-start(f32[768,3840]{1,0:T(8,128)} %wgrad_1_1.2.refs_3_), channel_id=1, source_target_pairs={{0,2},{1,3},{2,0},{3,1},{4,6},{5,7},{6,4},{7,5}} | collective-permute-start | bytes 35389448 | tf_op jit(solution)/shard_map/ppermute | solution.py:316
  1729.5 118.0 %collective-permute-start.22 = (f32[768,3840]{1,0:T(8,128)}, f32[768,3840]{1,0:T(8,128)}, u32[]{:S(2)}, u32[]{:S(2)}) collective-permute-start(f32[768,3840]{1,0:T(8,128)} %wgrad_0_0.6.refs_0_), channel_id=1, source_target_pairs={{0,1},{1,0},{2,3},{3,2},{4,5},{5,4},{6,7},{7,6}} | collective-permute-start | bytes 35389448 | tf_op jit(solution)/shard_map/ppermute | solution.py:315
  1788.2 130.3 %collective-permute-start.24 = (f32[768,3840]{1,0:T(8,128)}, f32[768,3840]{1,0:T(8,128)}, u32[]{:S(2)}, u32[]{:S(2)}) collective-permute-start(f32[768,3840]{1,0:T(8,128)} %wgrad_0_0.7.refs_0_), channel_id=1, source_target_pairs={{0,1},{1,0},{2,3},{3,2},{4,5},{5,4},{6,7},{7,6}} | collective-permute-start | bytes 35389448 | tf_op jit(solution)/shard_map/ppermute | solution.py:315
  1788.5 311.0 %collective-permute-start.25 = (f32[768,3840]{1,0:T(8,128)}, f32[768,3840]{1,0:T(8,128)}, u32[]{:S(2)}, u32[]{:S(2)}) collective-permute-start(f32[768,3840]{1,0:T(8,128)} %wgrad_1_1.3.refs_0_), channel_id=1, source_target_pairs={{0,2},{1,3},{2,0},{3,1},{4,6},{5,7},{6,4},{7,5}} | collective-permute-start | bytes 35389448 | tf_op jit(solution)/shard_map/ppermute | solution.py:316
  1912.9 253.6 %collective-permute-start.27 = (f32[768,3840]{1,0:T(8,128)}, f32[768,3840]{1,0:T(8,128)}, u32[]{:S(2)}, u32[]{:S(2)}) collective-permute-start(f32[768,3840]{1,0:T(8,128)} %wgrad_1_2.2.refs_0_), channel_id=1, source_target_pairs={{0,1},{2,3},{4,5},{6,7}} | collective-permute-start | bytes 35389448 | tf_op jit(solution)/shard_map/ppermute | solution.py:332
  2165.1 20.5 collective-permute-start.26
  2172.0 4.3 copy-start
  2176.2 9.4 slice-start
  2176.4 9.3 slice-start.1
  2176.4 9.3 slice-start.2
